TPU v7x, 32 devices: a whole 2x2x4 slice. The times are simulated.
32 devices in a mesh: gx: 16 (over z, y, core), gy: 2 (over x).
Axes of the slice: x: 2, y: 2, z: 4, core: 2. Of those that a mesh axis runs over, the one named last changes fastest.
Arguments:
- old_block: float32 [12288, 24576], P('gx', 'gy'), may hold values from -6 to 6
- vectors: bfloat16 [256, 2, 12288], P(None, 'gy', 'gx'), may hold values from -4 to 4
- prior: bfloat16 [32768, 3072], P('gx', 'gy'), may hold values from -2 to 2
- pair_columns: float32 [32768, 128], P(('gx', 'gy')), may hold values from -6 to 6
- pivots: int32 [128], replicated, may hold values from 0 to 32767
Outputs:
- new_block: float32 [12288, 24576], P('gx', 'gy')
- residual_columns: float32 [32768, 128], P(('gx', 'gy'))
Inputs may be any that keep to these rules, and one draw needn't show every extreme that they name: `pivots`: pivot AO-pair row indices, repeats possible.
All inputs are finite; a program needn't handle non-finite values.
Results may differ from a plain program's by a relative error of at most 0.0055.
Values may be sent and summed in bfloat16 or wider, within the bound.
No kernel may reach another device: no remote copies, remote signals or barrier semaphores. Data moves between devices by JAX's collectives and lax.ppermute only.
A program may use at most 192 MiB of HBM per device.

v0:
```python
import jax
import jax.numpy as jnp
from jax import lax
from jax.sharding import PartitionSpec as P


def from_root(value, axis, root):
    mine = lax.axis_index(axis) == root
    return lax.psum(jnp.where(mine, value, jnp.zeros_like(value)), axis)


def local(old_block, vectors, prior, pair_columns, pivots):
    local_vectors = vectors.reshape(vectors.shape[0], vectors.shape[2])
    slab_part = from_root(local_vectors, "gy", 0)
    gained = jnp.dot(
        slab_part.T,
        lax.all_gather(local_vectors, "gx", axis=1, tiled=True),
        preferred_element_type=jnp.float32,
    )
    new_block = old_block + gained
    rows_local = prior.shape[0]
    offset = lax.axis_index("gx") * rows_local
    local_index = pivots - offset
    inside = jnp.logical_and(local_index >= 0, local_index < rows_local)
    chosen = jnp.take(prior, jnp.clip(local_index, 0, rows_local - 1), axis=0).astype(jnp.float32)
    chosen = chosen * inside[:, None].astype(jnp.float32)
    pivot_block = lax.psum(chosen.astype(jnp.bfloat16), "gx")
    groups = lax.axis_size("gy")
    width = prior.shape[1]
    regrouped = lax.all_to_all(prior, "gy", split_axis=0, concat_axis=1, tiled=True)
    full_pivots = lax.all_gather(pivot_block, "gy", axis=1, tiled=True)
    parts = jnp.einsum(
        "rgc,kgc->grk",
        regrouped.reshape(regrouped.shape[0], groups, width),
        full_pivots.reshape(full_pivots.shape[0], groups, width),
        preferred_element_type=jnp.float32,
    )
    rounded = lax.optimization_barrier(parts.astype(jnp.bfloat16))
    intersection = jnp.sum(rounded.astype(jnp.float32), axis=0)
    return (new_block, pair_columns - intersection)


def solution(mesh):
    placed = (P("gx", "gy"), P(None, "gy", "gx"), P("gx", "gy"), P(("gx", "gy"), None), P())
    return jax.shard_map(
        local,
        mesh=mesh,
        in_specs=placed,
        out_specs=(P("gx", "gy"), P(("gx", "gy"), None)),
        check_vma=False,
    )
```

profile of v0, /device:TPU:0, one launch (start us, length us, event | category | flops | bytes accessed | tf_op | source)
XLA Modules:
  0.0 236.3 jit_solution(9439408910341760958)
XLA Ops:
  7.2 0.0 all-reduce.5.cloned.1.call-start
  7.2 0.7 compare_and_fusion
  7.9 4.8 %gather_fusion = bf16[128,1536]{1,0:T(8,128)(2,1)S(1)} fusion(bf16[2048,1536]{1,0:T(8,128)(2,1)} %param.7, s32[1024]{0:T(1024)S(1)} %pad_clamp_fusion), kind=kCustom, calls=%fused_computation | custom fusion | bytes 786944 | tf_op jit(solution)/shard_map/jit(_take)/gather | solution.py:25
  12.7 0.9 multiply_convert_fusion
  13.7 0.0 all-reduce.5.cloned.1.call-update
  13.7 0.0 all-reduce.3.cloned.1.call-start
  13.8 1.8 select_bitcast_fusion
  15.6 0.0 all-reduce.3.cloned.1.call-update
  15.6 0.0 all-gather.3.cloned.1.call-start
  15.6 0.7 all-gather.3.cloned.1.call-update
  16.3 0.0 copy-start
  16.3 6.5 %all-to-all-start = ((bf16[2,1024,1536]{2,1,0:T(8,128)(2,1)}), bf16[2,1024,1536]{2,1,0:T(8,128)(2,1)}, u32[]{:S(2)}, u32[]{:S(2)}) async-start(bf16[2,1024,1536]{2,1,0:T(8,128)(2,1)} %bitcast.18), calls=%async_computation | async-start | bytes 12582912 | tf_op jit(solution)/shard_map/all_to_all | solution.py:30
  22.8 0.0 copy-done
  22.8 0.2 copy.11
  23.0 84.9 %all-reduce.5.cloned.1.call-done = bf16[128,1536]{1,0:T(8,128)(2,1)} async-done(((bf16[128,1536]{1,0:T(8,128)(2,1)}), bf16[128,1536]{1,0:T(8,128)(2,1)}) %all-reduce.5.cloned.1.call-update) | async-done | bytes 393232 | tf_op jit(solution)/shard_map/psum | solution.py:27
  107.9 14.1 %all_gather.7 = bf16[128,3072]{1,0:T(8,128)(2,1)S(1)} all-gather(bf16[128,1536]{1,0:T(8,128)(2,1)} %all-reduce.5.cloned.1.call-done), channel_id=1, replica_groups=mesh['gx'=16,'gy'=2] {'gy'}, dimensions={1}, use_global_device_ids=true | all-gather | bytes 1179648 | tf_op jit(solution)/shard_map/all_gather | solution.py:31
  122.1 0.4 copy.9
  122.4 0.0 all-to-all-done
  122.4 5.0 %fusion.6 = bf16[2,1024,128]{1,2,0:T(8,128)(2,1)S(1)} fusion(bf16[128,2,1536]{0,2,1:T(8,128)(2,1)S(1)} %bitcast.19, bf16[2,1024,1536]{2,1,0:T(8,128)(2,1)} %all-to-all-done), kind=kOutput, calls=%fused_computation.6 | convolution fusion | flops 805568512 | bytes 7602176 | tf_op jit(solution)/shard_map/rgc,kgc->grk/dot_general | solution.py:32
  127.5 0.1 convert_reduce_fusion
  127.6 0.1 sub.11
  127.6 1.0 copy.12
  128.6 7.6 %all-reduce.3.cloned.1.call-done = bf16[256,768]{1,0:T(8,128)(2,1)} async-done(((bf16[256,768]{1,0:T(8,128)(2,1)}), bf16[256,768]{1,0:T(8,128)(2,1)}) %all-reduce.3.cloned.1.call-update) | async-done | bytes 393232 | tf_op jit(solution)/shard_map/psum | solution.py:9
  136.2 63.9 %all-gather.3.cloned.1.call-done = bf16[256,1,12288]{2,0,1:T(8,128)(2,1)} async-done(((bf16[256,1,768]{2,0,1:T(8,128)(2,1)}), bf16[256,1,12288]{2,0,1:T(8,128)(2,1)}) %all-gather.3.cloned.1.call-update) | async-done | bytes 6291472 | tf_op jit(solution)/shard_map/all_gather | solution.py:17
  200.1 29.6 %convolution_add_fusion = f32[768,12288]{1,0:T(8,128)} fusion(f32[768,12288]{1,0:T(8,128)} %param.5, bf16[256,768]{1,0:T(8,128)(2,1)} %all-reduce.3.cloned.1.call-done, bf16[256,1,12288]{2,0,1:T(8,128)(2,1)} %all-gather.3.cloned.1.call-done), kind=kOutput, calls=%fused_computation.1 | convolution fusion | flops 4841275392 | bytes 82182144 | tf_op jit(solution)/shard_map/dot_general | solution.py:15
  (1 shorter events, 0.0 us)
Async XLA Ops:
  7.2 100.7 %all-reduce.5.cloned.1.call-start = ((), (), s32[]{:S(2)}) async-start(), calls=%async_computation.2 | async-start | bytes 786432 | tf_op jit(solution)/shard_map/psum | solution.py:27
  13.7 122.5 %all-reduce.3.cloned.1.call-start = ((), (), s32[]{:S(2)}) async-start(), calls=%async_computation.1 | async-start | bytes 786432 | tf_op jit(solution)/shard_map/psum | solution.py:9
  15.6 184.5 %all-gather.3.cloned.1.call-start = ((), (), s32[]{:S(2)}) async-start(), calls=%async_computation.3 | async-start | bytes 6684672 | tf_op jit(solution)/shard_map/all_gather | solution.py:17
  16.3 6.5 %copy-start = (f32[1024,128]{1,0:T(8,128)S(1)}, f32[1024,128]{1,0:T(8,128)}, u32[]{:S(2)}) copy-start(f32[1024,128]{1,0:T(8,128)} %param.8) | copy-start | bytes 1572868
  16.3 106.1 %all-to-all-start = ((bf16[2,1024,1536]{2,1,0:T(8,128)(2,1)}), bf16[2,1024,1536]{2,1,0:T(8,128)(2,1)}, u32[]{:S(2)}, u32[]{:S(2)}) async-start(bf16[2,1024,1536]{2,1,0:T(8,128)(2,1)} %bitcast.18), calls=%async_computation | async-start | bytes 12582912 | tf_op jit(solution)/shard_map/all_to_all | solution.py:30
Sparse Core Ops, SparseCore 0:
  13.8 94.0 all-reduce.4
  110.8 25.4 all-reduce.2
  138.5 61.5 all-gather.2
where the time goes:
time: 237 us; the launch traced here: 236 us
  waiting for transfers between devices  157 us (66%)
  matrix products  34.7 us (15%)
  blocking collectives  14.1 us (6%)
  between operations  13.8 us (6%)
  starting transfers between devices  6.59 us (3%)
  local copies, waits for them, and re-layouts  6.42 us (3%)
  other arithmetic  3.57 us (2%)
    psum x1, waiting for transfers between devices, local(): pivot_block = lax.psum(chosen.astype(jnp.bfloat16), 'gx')  84.9 us
    all_gather x1, waiting for transfers between devices, local(): lax.all_gather(local_vectors, 'gx', axis=1, tiled=True)  63.9 us
    dot_general x1, matrix products, local(): jnp.dot(slab_part.T, lax.all_gather(local_vectors, 'gx', axis=1, tiled=Tr...  29.6 us
    all_gather x1, blocking collectives, local(): full_pivots = lax.all_gather(pivot_block, 'gy', axis=1, tiled=True)  14.1 us
    psum x1, waiting for transfers between devices, from_root(): return lax.psum(jnp.where(mine, value, jnp.zeros_like(value)), axis)  7.58 us
    all_to_all x1, starting transfers between devices, local(): lax.all_to_all(prior, 'gy', split_axis=0, concat_axis=1, tiled=True)  6.47 us
    dot_general x1, matrix products, local(): jnp.einsum('rgc,kgc->grk', regrouped.reshape(regrouped.shape[0], groups,...  5.02 us
    gather x1, local copies, waits for them, and re-layouts, local(): jnp.take(prior, jnp.clip(local_index, 0, rows_local - 1), axis=0)  4.85 us
  transfers between devices with their start and end apart: 4, of which 3 were waited for; matrix products, arithmetic and copies ran while one was open for 4% of the time, Pallas kernels for 0%

commit v1 on v0

--- a/solution.py
+++ b/solution.py
@@ -24,7 +24,9 @@
     inside = jnp.logical_and(local_index >= 0, local_index < rows_local)
     chosen = jnp.take(prior, jnp.clip(local_index, 0, rows_local - 1), axis=0).astype(jnp.float32)
     chosen = chosen * inside[:, None].astype(jnp.float32)
-    pivot_block = lax.psum(chosen.astype(jnp.bfloat16), "gx")
+    block = chosen.astype(jnp.bfloat16)
+    pieces = lax.all_gather(block, "gx")
+    pivot_block = jnp.sum(pieces, axis=0)
     groups = lax.axis_size("gy")
     width = prior.shape[1]
     regrouped = lax.all_to_all(prior, "gy", split_axis=0, concat_axis=1, tiled=True)

time: 237 us -> 179 us (0.76)
  waiting for transfers between devices: 157 us -> 79.5 us
  blocking collectives: 14.1 us -> 28.5 us
  other arithmetic: 3.57 us -> 7.35 us
    psum x1 -> x0, waiting for transfers between devices: 84.9 us -> none  [local(): pivot_block = lax.psum(chosen.astype(jnp.bfloat16), 'gx')]
    all_gather x0 -> x1, waiting for transfers between devices: none -> 55 us  [local(): pieces = lax.all_gather(block, 'gx')]
    all_gather x1, waiting for transfers between devices: 63.9 us -> 23.7 us  [local(): lax.all_gather(local_vectors, 'gx', axis=1, tiled=True)]
    all_gather x1, blocking collectives: 14.1 us -> 28.5 us  [local(): full_pivots = lax.all_gather(pivot_block, 'gy', axis=1, tiled=True)]
    psum x1, waiting for transfers between devices: 7.58 us -> 0.01 us  [from_root(): return lax.psum(jnp.where(mine, value, jnp.zeros_like(value)), axis)]
    reduce_sum x0 -> x1, other arithmetic: none -> 3.78 us  [local(): pivot_block = jnp.sum(pieces, axis=0)]
  transfers between devices with their start and end apart: 4 -> 4, of which waited for: 3 -> 2; matrix products, arithmetic and copies ran while one was open for 4% -> 7% of each run, Pallas kernels for 0% -> 0%
where the time goes in v1:
time: 179 us; the launch traced here: 178 us
  waiting for transfers between devices  79.5 us (44%)
  matrix products  34.6 us (19%)
  blocking collectives  28.5 us (16%)
  between operations  15.6 us (9%)
  other arithmetic  7.35 us (4%)
  starting transfers between devices  6.54 us (4%)
  local copies, waits for them, and re-layouts  6.42 us (4%)
    all_gather x1, waiting for transfers between devices, local(): pieces = lax.all_gather(block, 'gx')  55 us
    dot_general x1, matrix products, local(): jnp.dot(slab_part.T, lax.all_gather(local_vectors, 'gx', axis=1, tiled=Tr...  29.6 us
    all_gather x1, blocking collectives, local(): full_pivots = lax.all_gather(pivot_block, 'gy', axis=1, tiled=True)  28.5 us
    all_gather x1, waiting for transfers between devices, local(): lax.all_gather(local_vectors, 'gx', axis=1, tiled=True)  23.7 us
    all_to_all x1, starting transfers between devices, local(): lax.all_to_all(prior, 'gy', split_axis=0, concat_axis=1, tiled=True)  6.41 us
    dot_general x1, matrix products, local(): jnp.einsum('rgc,kgc->grk', regrouped.reshape(regrouped.shape[0], groups,...  4.98 us
    gather x1, local copies, waits for them, and re-layouts, local(): jnp.take(prior, jnp.clip(local_index, 0, rows_local - 1), axis=0)  4.85 us
    reduce_sum x1, other arithmetic, local(): pivot_block = jnp.sum(pieces, axis=0)  3.78 us
  transfers between devices with their start and end apart: 4, of which 2 were waited for; matrix products, arithmetic and copies ran while one was open for 7% of the time, Pallas kernels for 0%

profile of v1, /device:TPU:0, one launch (start us, length us, event | category | flops | bytes accessed | tf_op | source)
XLA Modules:
  0.0 178.5 jit_solution(13651474671282826932)
XLA Ops:
  8.0 0.0 all-gather.4.cloned.1.call-start
  8.0 0.7 compare_and_fusion
  8.7 4.8 %gather_fusion = bf16[128,1536]{1,0:T(8,128)(2,1)S(1)} fusion(bf16[2048,1536]{1,0:T(8,128)(2,1)} %param.7, s32[1024]{0:T(1024)S(1)} %pad_clamp_fusion), kind=kCustom, calls=%fused_computation | custom fusion | bytes 786944 | tf_op jit(solution)/shard_map/jit(_take)/gather | solution.py:25
  13.6 0.9 multiply_convert_fusion
  14.5 0.0 all-gather.4.cloned.1.call-update
  14.6 0.0 all-reduce.2.cloned.1.call-start
  14.6 1.8 select_bitcast_fusion
  16.4 0.0 all-reduce.2.cloned.1.call-update
  16.4 0.0 all-gather.6.cloned.1.call-start
  16.5 0.7 all-gather.6.cloned.1.call-update
  17.2 0.0 copy-start
  17.2 6.4 %all-to-all-start = ((bf16[2,1024,1536]{2,1,0:T(8,128)(2,1)}), bf16[2,1024,1536]{2,1,0:T(8,128)(2,1)}, u32[]{:S(2)}, u32[]{:S(2)}) async-start(bf16[2,1024,1536]{2,1,0:T(8,128)(2,1)} %bitcast.22), calls=%async_computation | async-start | bytes 12582912 | tf_op jit(solution)/shard_map/all_to_all | solution.py:32
  23.6 0.0 copy-done
  23.6 0.2 copy.10
  23.8 55.0 %all-gather.4.cloned.1.call-done = bf16[16,128,1536]{2,1,0:T(8,128)(2,1)} async-done(((bf16[1,128,1536]{2,1,0:T(8,128)(2,1)}), bf16[16,128,1536]{2,1,0:T(8,128)(2,1)}) %all-gather.4.cloned.1.call-update) | async-done | bytes 6291472 | tf_op jit(solution)/shard_map/all_gather | solution.py:28
  78.8 3.8 %reduce_sum.21 = bf16[128,1536]{1,0:T(8,128)(2,1)S(1)} reduce(bf16[16,128,1536]{2,1,0:T(8,128)(2,1)} %all-gather.4.cloned.1.call-done, bf16[]{:T(256)} %constant.12.clone.1), dimensions={0}, to_apply=%region_1.2 | reduce | flops 2949120 | bytes 6684674 | tf_op jit(solution)/shard_map/reduce_sum | solution.py:29
  82.6 28.5 %all_gather.12 = bf16[128,3072]{1,0:T(8,128)(2,1)S(1)} all-gather(bf16[128,1536]{1,0:T(8,128)(2,1)S(1)} %reduce_sum.21), channel_id=1, replica_groups=mesh['gx'=16,'gy'=2] {'gy'}, dimensions={1}, use_global_device_ids=true | all-gather | bytes 1179648 | tf_op jit(solution)/shard_map/all_gather | solution.py:33
  111.1 0.4 copy.8
  111.5 0.0 all-to-all-done
  111.5 5.0 %fusion.6 = bf16[2,1024,128]{1,2,0:T(8,128)(2,1)S(1)} fusion(bf16[128,2,1536]{0,2,1:T(8,128)(2,1)S(1)} %bitcast.23, bf16[2,1024,1536]{2,1,0:T(8,128)(2,1)} %all-to-all-done), kind=kOutput, calls=%fused_computation.6 | convolution fusion | flops 805568512 | bytes 7602176 | tf_op jit(solution)/shard_map/rgc,kgc->grk/dot_general | solution.py:34
  116.5 0.1 convert_reduce_fusion
  116.6 0.1 sub.11
  116.7 1.0 copy.11
  117.7 0.0 all-reduce.2.cloned.1.call-done
  117.7 23.7 %all-gather.6.cloned.1.call-done = bf16[256,1,12288]{2,0,1:T(8,128)(2,1)} async-done(((bf16[256,1,768]{2,0,1:T(8,128)(2,1)}), bf16[256,1,12288]{2,0,1:T(8,128)(2,1)}) %all-gather.6.cloned.1.call-update) | async-done | bytes 6291472 | tf_op jit(solution)/shard_map/all_gather | solution.py:17
  141.4 29.6 %convolution_add_fusion = f32[768,12288]{1,0:T(8,128)} fusion(f32[768,12288]{1,0:T(8,128)} %param.5, bf16[256,768]{1,0:T(8,128)(2,1)} %all-reduce.2.cloned.1.call-done, bf16[256,1,12288]{2,0,1:T(8,128)(2,1)} %all-gather.6.cloned.1.call-done), kind=kOutput, calls=%fused_computation.1 | convolution fusion | flops 4841275392 | bytes 82182144 | tf_op jit(solution)/shard_map/dot_general | solution.py:15
  (1 shorter events, 0.0 us)
Async XLA Ops:
  8.0 70.8 %all-gather.4.cloned.1.call-start = ((), (), s32[]{:S(2)}) async-start(), calls=%async_computation.2 | async-start | bytes 6684672 | tf_op jit(solution)/shard_map/all_gather | solution.py:28
  14.6 103.1 %all-reduce.2.cloned.1.call-start = ((), (), s32[]{:S(2)}) async-start(), calls=%async_computation.1 | async-start | bytes 786432 | tf_op jit(solution)/shard_map/psum | solution.py:9
  16.4 125.0 %all-gather.6.cloned.1.call-start = ((), (), s32[]{:S(2)}) async-start(), calls=%async_computation.3 | async-start | bytes 6684672 | tf_op jit(solution)/shard_map/all_gather | solution.py:17
  17.2 6.4 %copy-start = (f32[1024,128]{1,0:T(8,128)S(1)}, f32[1024,128]{1,0:T(8,128)}, u32[]{:S(2)}) copy-start(f32[1024,128]{1,0:T(8,128)} %param.8) | copy-start | bytes 1572868
  17.2 94.3 %all-to-all-start = ((bf16[2,1024,1536]{2,1,0:T(8,128)(2,1)}), bf16[2,1024,1536]{2,1,0:T(8,128)(2,1)}, u32[]{:S(2)}, u32[]{:S(2)}) async-start(bf16[2,1024,1536]{2,1,0:T(8,128)(2,1)} %bitcast.22), calls=%async_computation | async-start | bytes 12582912 | tf_op jit(solution)/shard_map/all_to_all | solution.py:32
Sparse Core Ops, SparseCore 0:
  14.7 64.1 all-gather.3
  81.1 60.2 all-gather.5
Sparse Core Ops, SparseCore 1:
  17.9 37.0 all-reduce.1
